TPU v7x, 32 devices: a whole 2x2x4 slice. The times are simulated.
32 devices in a mesh: batch: 8 (over y, x, core), head: 4 (over z).
Axes of the slice: x: 2, y: 2, z: 4, core: 2. Of those that a mesh axis runs over, the one named last changes fastest.
Arguments:
- inputs: bfloat16 [8, 128, 2048], P(None, 'batch', 'head'), parts along dimension 1, may hold values from -6 to 6
- in_weight: bfloat16 [2048, 4, 384], P(None, 'head'), may hold values from -0.125 to 0.125
- gate_weight: bfloat16 [2048, 4], P(None, 'head'), may hold values from -0.125 to 0.125
- gate_bias: float32 [4], P('head'), may hold values from -2 to 3
- norm_gain: float32 [512], P('head'), may hold values from 0.1 to 1.9
- out_weight: bfloat16 [512, 2048], P('head'), may hold values from -0.375 to 0.375
- inv_gram: float32 [128, 4, 128, 128], P('batch', 'head'), parts along dimension 0, may hold values from -17 to 17, as said below
- value_key: float32 [128, 4, 128, 128], P('batch', 'head'), parts along dimension 0, may hold values from -6 to 6
Outputs:
- layer_out: float32 [8, 128, 2048], P(None, 'batch', 'head'), parts along dimension 1
There are 8 independent parts, one for each index of `batch`. A program takes and returns all parts, laid end to end along the dimension named above; an argument that names none is the same for every part. Nothing has to cross between parts.
Inputs may be any that keep to these rules, and one draw needn't show every extreme that they name: `inv_gram`: each [128, 128] matrix is symmetric positive definite.
All inputs are finite; a program needn't handle non-finite values.
Results may differ from a plain program's by a relative error of at most 0.0029.
Values may be sent and summed in bfloat16 or wider, within the bound.
No kernel may reach another device: no remote copies, remote signals or barrier semaphores. Data moves between devices by JAX's collectives and lax.ppermute only.
A program may use at most 64 MiB of HBM per device.

v0:
```python
import functools

import jax
import jax.numpy as jnp
from jax import lax
from jax.experimental import pallas as pl
from jax.experimental.pallas import tpu as pltpu
from jax.sharding import PartitionSpec as P


EPS = 1e-06
VMEM_BYTES = 16 * 2**20


def dot(a, b, dims=((1,), (0,))):
    return lax.dot_general(a, b, (dims, ((), ())), preferred_element_type=jnp.float32)


def lane_sum(a):
    return jnp.sum(a, axis=-1, keepdims=True)


def split(a):
    high = a.astype(jnp.bfloat16)
    return high, (a - high.astype(jnp.float32)).astype(jnp.bfloat16)


def partner(index, shift, size):
    return index ^ shift if size & (size - 1) == 0 else (index + shift) % size


def source(index, shift, size):
    return index ^ shift if size & (size - 1) == 0 else (index - shift) % size


def shift_order(size):
    return [*range(size // 2, size), *range(1, size // 2)]


def exchange(arrays, size):
    got = {}
    for s in shift_order(size):
        got[s] = lax.ppermute(arrays[s], "head", [(i, partner(i, s, size)) for i in range(size)])
    return [got[s] for s in range(1, size)]


def call(kernel, out_shape, scratch=()):
    return pl.pallas_call(
        kernel,
        out_shape=out_shape,
        scratch_shapes=[pltpu.VMEM(shape, dtype) for shape, dtype in scratch],
        compiler_params=pltpu.CompilerParams(vmem_limit_bytes=VMEM_BYTES),
    )


def pack_kernel(gram_ref, memory_ref, gram_out, memory_out):
    pairs, width, _ = gram_out.shape
    size = width // 2
    for p in range(pairs):
        for i in range(2):
            high, low = split(gram_ref[2 * p + i])
            gram_out[p, :size, i * size : (i + 1) * size] = high
            gram_out[p, size:, i * size : (i + 1) * size] = low
            high, low = split(memory_ref[2 * p + i])
            memory_out[p, i * size : (i + 1) * size, :size] = high
            memory_out[p, i * size : (i + 1) * size, size:] = low


def slice_kernel(shards, weight_ref, own_ref, *piece_refs):
    me = lax.axis_index("head")
    half, cols = piece_refs[0].shape
    mine = pl.multiple_of((lax.axis_index("batch") % 2) * half, half)
    own_ref[...] = weight_ref[:, pl.ds(pl.multiple_of(me * cols, cols), cols)]
    for s in range(1, shards):
        off = pl.multiple_of(partner(me, s, shards) * cols, cols)
        piece_refs[s - 1][...] = weight_ref[pl.ds(mine, half), pl.ds(off, cols)]


def join_kernel(*refs):
    half = refs[0].shape[0]
    for s, ref in enumerate(refs[:-1]):
        refs[-1][s * half : (s + 1) * half] = ref[...]


def mesa_kernel(shards, steps, *refs):
    x_refs = refs[:shards]
    w_ref, gate_ref, bias_ref, gain_ref, gram_ref, memory_ref, out_ref, kq, ab, xs, ys = refs[shards:]
    rows, features = x_refs[0].shape
    seqs = rows // steps
    size = out_ref.shape[1]
    me = lax.axis_index("head")
    projected = 0.0
    gate = 0.0
    for s in range(shards):
        off = pl.multiple_of(source(me, s, shards) * features, features)
        projected = projected + dot(x_refs[s][...], w_ref[pl.ds(off, features), :])
        gate_rows = jnp.broadcast_to(gate_ref[:, pl.ds(off, features)], (size, features))
        gate = gate + dot(x_refs[s][...], gate_rows, ((1,), (1,)))
    forget = 0.8 + 0.2 * jax.nn.sigmoid(gate + bias_ref[...])
    queries = projected[:, :size]
    keys = projected[:, size : 2 * size]
    values = projected[:, 2 * size :]
    keys = keys * lax.rsqrt(lane_sum(keys * keys) + EPS)
    queries = queries * lax.rsqrt(lane_sum(queries * queries) + EPS)
    kq[:rows] = keys
    kq[rows:] = queries
    for p in range(seqs // 2):
        parts = []
        for i in range(2):
            parts += split(kq[pl.ds(2 * p + i, 2 * steps, stride=seqs), :])
        lhs = jnp.concatenate(parts, axis=0)
        res = dot(jnp.concatenate([lhs, lhs], axis=1), gram_ref[p])
        for i in range(2):
            half = res[i * 4 * steps : (i + 1) * 4 * steps, i * size : (i + 1) * size]
            ab[pl.ds(2 * p + i, 2 * steps, stride=seqs), :] = half[: 2 * steps] + half[2 * steps :]

    def at(array, t):
        return array[t * seqs : (t + 1) * seqs]

    k = [at(keys, t) for t in range(steps)]
    q = [at(queries, t) for t in range(steps)]
    a = [ab[t * seqs : (t + 1) * seqs, :] for t in range(steps)]
    b = [ab[rows + t * seqs : rows + (t + 1) * seqs, :] for t in range(steps)]
    decay = []
    for t in range(steps):
        decay.append(at(forget, t) if t == 0 else decay[-1] * at(forget, t))
    for s in range(steps):
        g = a[s]
        u = g / (decay[s] + lane_sum(g * k[s]))
        for t in range(s + 1, steps):
            a[t] = a[t] - u * lane_sum(g * k[t])
        for t in range(s, steps):
            b[t] = b[t] - u * lane_sum(g * q[t])
    for t in range(steps):
        xs[t * seqs : (t + 1) * seqs, :] = b[t]
    for p in range(seqs // 2):
        parts = []
        for i in range(2):
            parts += split(xs[pl.ds(2 * p + i, steps, stride=seqs), :])
        lhs = jnp.concatenate(parts, axis=0)
        res = dot(jnp.concatenate([lhs, lhs], axis=1), memory_ref[p], ((1,), (1,)))
        for i in range(2):
            half = res[i * 2 * steps : (i + 1) * 2 * steps, i * size : (i + 1) * size]
            ys[pl.ds(2 * p + i, steps, stride=seqs), :] = half[:steps] + half[steps:]
    scaled = [at(values, t) / decay[t] for t in range(steps)]
    for t in range(steps):
        y = ys[t * seqs : (t + 1) * seqs, :]
        for s in range(t + 1):
            y = y + scaled[s] * lane_sum(k[s] * b[t])
        out_ref[t * seqs : (t + 1) * seqs, :] = y
    out_ref[rows:, :] = jnp.broadcast_to(gain_ref[...], (out_ref.shape[0] - rows, size))


def output_kernel(shards, *refs):
    r_refs = refs[:shards]
    own_ref = refs[shards]
    mine_ref, other_ref, out_ref, w_scr = refs[shards + 1 :]
    rows = out_ref.shape[0]
    half = mine_ref.shape[0] // (shards - 1)
    width = own_ref.shape[0]
    mine = pl.multiple_of((lax.axis_index("batch") % 2) * half, half)
    other = pl.multiple_of(half - mine, half)
    w_scr[:width] = own_ref[...]
    for s in range(1, shards):
        w_scr[pl.ds(s * width + mine, half), :] = mine_ref[(s - 1) * half : s * half]
        w_scr[pl.ds(s * width + other, half), :] = other_ref[(s - 1) * half : s * half]
    size = r_refs[0].shape[1]
    total = 0.0
    for s in range(shards):
        r = r_refs[s][:rows]
        total = total + lane_sum(r * r)
    scale = lax.rsqrt(total / (size * shards) + EPS)
    hidden = [(r[rows : rows + 1] * r[:rows] * scale).astype(jnp.bfloat16) for r in r_refs]
    out_ref[...] = dot(jnp.concatenate(hidden, axis=1), w_scr[...])


def local(inputs, in_weight, gate_weight, gate_bias, norm_gain, out_weight, inv_gram, value_key):
    steps, seqs, features = inputs.shape
    d_model, local_heads, width = in_weight.shape
    assert local_heads == 1 and seqs % 2 == 0 and lax.axis_size("batch") % 2 == 0
    size = width // 3
    rows = steps * seqs
    shards = lax.axis_size("head")
    out_cols = out_weight.shape[1] // shards
    x = inputs.reshape(rows, features)
    groups = lax.axis_size("batch")
    half = size // 2
    xs = [x] + exchange([x] * shards, shards)
    piece = jax.ShapeDtypeStruct((half, out_cols), jnp.bfloat16)
    w_own, *ws = call(
        functools.partial(slice_kernel, shards),
        [jax.ShapeDtypeStruct((size, out_cols), jnp.bfloat16)] + [piece] * (shards - 1),
    )(out_weight)
    ws = exchange([None, *ws], shards)
    weight = in_weight.reshape(d_model, width)
    tiles = jax.ShapeDtypeStruct((seqs // 2, 2 * size, 2 * size), jnp.bfloat16)
    gram, memory = call(pack_kernel, (tiles, tiles))(
        inv_gram.reshape(seqs, size, size), value_key.reshape(seqs, size, size)
    )
    readout = call(
        functools.partial(mesa_kernel, shards, steps),
        jax.ShapeDtypeStruct((rows + 8, size), jnp.float32),
        [((2 * rows, size), jnp.float32)] * 2 + [((rows, size), jnp.float32)] * 2,
    )(*xs, weight, gate_weight.reshape(1, d_model), gate_bias.reshape(1, 1), norm_gain.reshape(1, size), gram, memory)
    rs = [readout] + exchange([readout] * shards, shards)
    w_mine = call(join_kernel, jax.ShapeDtypeStruct(((shards - 1) * half, out_cols), jnp.bfloat16))(*ws)
    w_other = lax.ppermute(w_mine, "batch", [(i, i ^ 1) for i in range(groups)])
    out = call(
        functools.partial(output_kernel, shards),
        jax.ShapeDtypeStruct((rows, out_cols), jnp.float32),
        [((shards * size, out_cols), jnp.bfloat16)],
    )(*rs, w_own, w_mine, w_other)
    return out.reshape(steps, seqs, out_cols)


def solution(mesh):
    in_specs = (
        P(None, "batch", "head"),
        P(None, "head", None),
        P(None, "head"),
        P("head"),
        P("head"),
        P("head", None),
        P("batch", "head", None, None),
        P("batch", "head", None, None),
    )
    out_specs = P(None, "batch", "head")
    return jax.shard_map(local, mesh=mesh, in_specs=in_specs, out_specs=out_specs, check_vma=False)
```

profile of v0, /device:TPU:0, one launch (start us, length us, event | category | flops | bytes accessed | tf_op | source)
XLA Modules:
  0.0 36.4 jit_solution(12270639454503257771)
XLA Ops:
  0.0 0.0 copy-start
  0.0 0.0 copy-start.3
  0.0 1.2 %copy-done.3 = bf16[128,2048]{1,0:T(8,128)(2,1)S(1)} copy-done((bf16[128,2048]{1,0:T(8,128)(2,1)S(1)}, bf16[128,2048]{1,0:T(8,128)(2,1)}, u32[]{:S(2)}) %copy-start.3) | copy-done | bytes 524312
  1.2 3.1 %collective-permute-start.6 = (bf16[64,512]{1,0:T(8,128)(2,1)S(1)}, bf16[64,512]{1,0:T(8,128)(2,1)S(1)}, u32[]{:S(2)}, u32[]{:S(2)}) collective-permute-start(bf16[64,512]{1,0:T(8,128)(2,1)S(1)} %get-tuple-element.14), channel_id=1, source_target_pairs={{0,1},{1,0},{2,3},{3,2},{4,5},{5,4},{6,7},{7,6},{8,9},{9,8},{10,11... | collective-permute-start | bytes 196616 | tf_op jit(solution)/shard_map/ppermute | solution.py:43
  4.3 2.6 %collective-permute-start.7 = (bf16[64,512]{1,0:T(8,128)(2,1)S(1)}, bf16[64,512]{1,0:T(8,128)(2,1)S(1)}, u32[]{:S(2)}, u32[]{:S(2)}) collective-permute-start(bf16[64,512]{1,0:T(8,128)(2,1)S(1)} %get-tuple-element.15), channel_id=1, source_target_pairs={{0,2},{1,3},{2,0},{3,1},{4,6},{5,7},{6,4},{7,5},{8,10},{9,11},{10,... | collective-permute-start | bytes 196616 | tf_op jit(solution)/shard_map/ppermute | solution.py:43
  6.9 0.0 collective-permute-start.8
  6.9 0.9 %collective-permute-start = (bf16[128,512]{1,0:T(8,128)(2,1)}, bf16[128,512]{1,0:T(8,128)(2,1)S(1)}, u32[]{:S(2)}, u32[]{:S(2)}) collective-permute-start(bf16[128,512]{1,0:T(8,128)(2,1)} %bitcast.12), channel_id=1, source_target_pairs={{0,1},{1,0},{2,3},{3,2},{4,5},{5,4},{6,7},{7,6},{8,9},{9,8},{10,11... | collective-permute-start | bytes 393224 | tf_op jit(solution)/shard_map/ppermute | solution.py:43
  7.8 3.5 %collective-permute-start.1 = (bf16[128,512]{1,0:T(8,128)(2,1)}, bf16[128,512]{1,0:T(8,128)(2,1)S(1)}, u32[]{:S(2)}, u32[]{:S(2)}) collective-permute-start(bf16[128,512]{1,0:T(8,128)(2,1)} %bitcast.13), channel_id=1, source_target_pairs={{0,2},{1,3},{2,0},{3,1},{4,6},{5,7},{6,4},{7,5},{8,10},{9,11},{10,... | collective-permute-start | bytes 393224 | tf_op jit(solution)/shard_map/ppermute | solution.py:43
  11.3 0.0 collective-permute-done.6.refs_0_
  11.3 0.0 collective-permute-start.2
  11.3 0.3 collective-permute-done.7.refs_1_
  11.6 2.1 %collective-permute-done.8.refs_2_ = bf16[64,512]{1,0:T(8,128)(2,1)S(1)} collective-permute-done((bf16[64,512]{1,0:T(8,128)(2,1)S(1)}, bf16[64,512]{1,0:T(8,128)(2,1)S(1)}, u32[]{:S(2)}, u32[]{:S(2)}) %collective-permute-start.8) | collective-permute-done | bytes 65568 | tf_op jit(solution)/shard_map/ppermute | solution.py:43
  13.8 0.1 collective-permute-start.9
  14.5 0.0 copy-start.1
  14.5 1.2 %copy-done.1 = f32[16,1,128,128]{3,2,1,0:T(8,128)S(1)} copy-done((f32[16,1,128,128]{3,2,1,0:T(8,128)S(1)}, f32[16,1,128,128]{3,2,1,0:T(8,128)}, u32[]{:S(2)}) %copy-start.1) | copy-done | bytes 1048600
  15.7 0.0 copy-start.2
  15.7 1.2 %copy-done.2 = f32[16,1,128,128]{3,2,1,0:T(8,128)S(1)} copy-done((f32[16,1,128,128]{3,2,1,0:T(8,128)S(1)}, f32[16,1,128,128]{3,2,1,0:T(8,128)}, u32[]{:S(2)}) %copy-start.2) | copy-done | bytes 1048600
  17.0 0.0 copy-start.4
  17.0 0.0 copy-start.5
  17.0 0.0 copy-start.6
  17.0 0.3 shard_map.82
  17.3 0.0 collective-permute-done.refs_1_
  17.3 4.8 %collective-permute-done.1.refs_2_ = bf16[128,512]{1,0:T(8,128)(2,1)S(1)} collective-permute-done((bf16[128,512]{1,0:T(8,128)(2,1)}, bf16[128,512]{1,0:T(8,128)(2,1)S(1)}, u32[]{:S(2)}, u32[]{:S(2)}) %collective-permute-start.1) | collective-permute-done | bytes 131104 | tf_op jit(solution)/shard_map/ppermute | solution.py:43
  22.2 0.0 collective-permute-done.2.refs_3_
  22.2 0.0 copy-done
  22.2 0.0 copy-done.4
  22.2 0.0 copy-done.5
  22.2 0.0 copy-done.6
  22.2 2.0 %shard_map.83.refs_0_ = f32[136,128]{1,0:T(8,128)S(1)} custom-call(bf16[128,512]{1,0:T(8,128)(2,1)S(1)} %bitcast.15, bf16[128,512]{1,0:T(8,128)(2,1)S(1)} %collective-permute-done.refs_1_, bf16[128,512]{1,0:T(8,128)(2,1)S(1)} %collective-permute-done.1.refs_2_, bf16[128,512]{1,0:T(8,128)(2,1)S(1)} %collective-permute-done.2.refs_3_, ...), custom_call_target="tpu_custom_call" | custom-call | tf_op jit(solution)/shard_map/pallas_call | solution.py:200
  24.1 2.7 %collective-permute-start.3 = (f32[136,128]{1,0:T(8,128)S(1)}, f32[136,128]{1,0:T(8,128)S(1)}, u32[]{:S(2)}, u32[]{:S(2)}) collective-permute-start(f32[136,128]{1,0:T(8,128)S(1)} %shard_map.83.refs_0_), channel_id=1, source_target_pairs={{0,1},{1,0},{2,3},{3,2},{4,5},{5,4},{6,7},{7,6},{8,9},{9,8},{10,11... | collective-permute-start | bytes 208904 | tf_op jit(solution)/shard_map/ppermute | solution.py:43
  26.8 1.1 %collective-permute-start.4 = (f32[136,128]{1,0:T(8,128)S(1)}, f32[136,128]{1,0:T(8,128)S(1)}, u32[]{:S(2)}, u32[]{:S(2)}) collective-permute-start(f32[136,128]{1,0:T(8,128)S(1)} %shard_map.83.refs_0_), channel_id=1, source_target_pairs={{0,2},{1,3},{2,0},{3,1},{4,6},{5,7},{6,4},{7,5},{8,10},{9,11},{10,... | collective-permute-start | bytes 208904 | tf_op jit(solution)/shard_map/ppermute | solution.py:43
  28.0 1.4 %collective-permute-start.5 = (f32[136,128]{1,0:T(8,128)S(1)}, f32[136,128]{1,0:T(8,128)S(1)}, u32[]{:S(2)}, u32[]{:S(2)}) collective-permute-start(f32[136,128]{1,0:T(8,128)S(1)} %shard_map.83.refs_0_), channel_id=1, source_target_pairs={{0,3},{1,2},{2,1},{3,0},{4,7},{5,6},{6,5},{7,4},{8,11},{9,10},{10,... | collective-permute-start | bytes 208904 | tf_op jit(solution)/shard_map/ppermute | solution.py:43
  29.4 0.0 collective-permute-done.3.refs_1_
  29.4 6.0 %collective-permute-done.4.refs_2_ = f32[136,128]{1,0:T(8,128)S(1)} collective-permute-done((f32[136,128]{1,0:T(8,128)S(1)}, f32[136,128]{1,0:T(8,128)S(1)}, u32[]{:S(2)}, u32[]{:S(2)}) %collective-permute-start.4) | collective-permute-done | bytes 69664 | tf_op jit(solution)/shard_map/ppermute | solution.py:43
  35.3 0.0 collective-permute-done.5.refs_3_
  35.3 0.0 collective-permute-done.9.refs_6_
  35.3 1.0 %shard_map.86 = f32[128,512]{1,0:T(8,128)} custom-call(f32[136,128]{1,0:T(8,128)S(1)} %shard_map.83.refs_0_, f32[136,128]{1,0:T(8,128)S(1)} %collective-permute-done.3.refs_1_, f32[136,128]{1,0:T(8,128)S(1)} %collective-permute-done.4.refs_2_, f32[136,128]{1,0:T(8,128)S(1)} %collective-permute-done.5.refs_3_, ...), custom_call_target="tpu_custom_call" | custom-call | tf_op jit(solution)/shard_map/pallas_call | solution.py:208
  (2 shorter events, 0.0 us)
Async XLA Ops:
  0.0 22.2 %copy-start = (bf16[2048,1,384]{2,0,1:T(8,128)(2,1)S(1)}, bf16[2048,1,384]{2,0,1:T(8,128)(2,1)}, u32[]{:S(2)}) copy-start(bf16[2048,1,384]{2,0,1:T(8,128)(2,1)} %param.9) | copy-start | bytes 4718596
  0.0 1.2 %copy-start.3 = (bf16[128,2048]{1,0:T(8,128)(2,1)S(1)}, bf16[128,2048]{1,0:T(8,128)(2,1)}, u32[]{:S(2)}) copy-start(bf16[128,2048]{1,0:T(8,128)(2,1)} %weight_ref.1) | copy-start | bytes 1572868
  1.2 10.1 %collective-permute-start.6 = (bf16[64,512]{1,0:T(8,128)(2,1)S(1)}, bf16[64,512]{1,0:T(8,128)(2,1)S(1)}, u32[]{:S(2)}, u32[]{:S(2)}) collective-permute-start(bf16[64,512]{1,0:T(8,128)(2,1)S(1)} %get-tuple-element.14), channel_id=1, source_target_pairs={{0,1},{1,0},{2,3},{3,2},{4,5},{5,4},{6,7},{7,6},{8,9},{9,8},{10,11... | collective-permute-start | bytes 196616 | tf_op jit(solution)/shard_map/ppermute | solution.py:43
  4.3 7.3 %collective-permute-start.7 = (bf16[64,512]{1,0:T(8,128)(2,1)S(1)}, bf16[64,512]{1,0:T(8,128)(2,1)S(1)}, u32[]{:S(2)}, u32[]{:S(2)}) collective-permute-start(bf16[64,512]{1,0:T(8,128)(2,1)S(1)} %get-tuple-element.15), channel_id=1, source_target_pairs={{0,2},{1,3},{2,0},{3,1},{4,6},{5,7},{6,4},{7,5},{8,10},{9,11},{10,... | collective-permute-start | bytes 196616 | tf_op jit(solution)/shard_map/ppermute | solution.py:43
  6.9 6.9 %collective-permute-start.8 = (bf16[64,512]{1,0:T(8,128)(2,1)S(1)}, bf16[64,512]{1,0:T(8,128)(2,1)S(1)}, u32[]{:S(2)}, u32[]{:S(2)}) collective-permute-start(bf16[64,512]{1,0:T(8,128)(2,1)S(1)} %get-tuple-element.16), channel_id=1, source_target_pairs={{0,3},{1,2},{2,1},{3,0},{4,7},{5,6},{6,5},{7,4},{8,11},{9,10},{10,... | collective-permute-start | bytes 196616 | tf_op jit(solution)/shard_map/ppermute | solution.py:43
  6.9 10.4 %collective-permute-start = (bf16[128,512]{1,0:T(8,128)(2,1)}, bf16[128,512]{1,0:T(8,128)(2,1)S(1)}, u32[]{:S(2)}, u32[]{:S(2)}) collective-permute-start(bf16[128,512]{1,0:T(8,128)(2,1)} %bitcast.12), channel_id=1, source_target_pairs={{0,1},{1,0},{2,3},{3,2},{4,5},{5,4},{6,7},{7,6},{8,9},{9,8},{10,11... | collective-permute-start | bytes 393224 | tf_op jit(solution)/shard_map/ppermute | solution.py:43
  7.8 14.4 %collective-permute-start.1 = (bf16[128,512]{1,0:T(8,128)(2,1)}, bf16[128,512]{1,0:T(8,128)(2,1)S(1)}, u32[]{:S(2)}, u32[]{:S(2)}) collective-permute-start(bf16[128,512]{1,0:T(8,128)(2,1)} %bitcast.13), channel_id=1, source_target_pairs={{0,2},{1,3},{2,0},{3,1},{4,6},{5,7},{6,4},{7,5},{8,10},{9,11},{10,... | collective-permute-start | bytes 393224 | tf_op jit(solution)/shard_map/ppermute | solution.py:43
  11.3 10.9 %collective-permute-start.2 = (bf16[128,512]{1,0:T(8,128)(2,1)}, bf16[128,512]{1,0:T(8,128)(2,1)S(1)}, u32[]{:S(2)}, u32[]{:S(2)}) collective-permute-start(bf16[128,512]{1,0:T(8,128)(2,1)} %bitcast.14), channel_id=1, source_target_pairs={{0,3},{1,2},{2,1},{3,0},{4,7},{5,6},{6,5},{7,4},{8,11},{9,10},{10,... | collective-permute-start | bytes 393224 | tf_op jit(solution)/shard_map/ppermute | solution.py:43
  13.8 21.6 %collective-permute-start.9 = (bf16[192,512]{1,0:T(8,128)(2,1)S(1)}, bf16[192,512]{1,0:T(8,128)(2,1)S(1)}, u32[]{:S(2)}, u32[]{:S(2)}) collective-permute-start(bf16[192,512]{1,0:T(8,128)(2,1)S(1)} %shard_map.85.refs_5_), channel_id=1, source_target_pairs={{0,4},{4,0},{8,12},{12,8},{16,20},{20,16},{24,28},{28,24},{1,5},{5... | collective-permute-start | bytes 589832 | tf_op jit(solution)/shard_map/ppermute | solution.py:207
  14.5 1.2 %copy-start.1 = (f32[16,1,128,128]{3,2,1,0:T(8,128)S(1)}, f32[16,1,128,128]{3,2,1,0:T(8,128)}, u32[]{:S(2)}) copy-start(f32[16,1,128,128]{3,2,1,0:T(8,128)} %param.14) | copy-start | bytes 3145732
  15.7 1.2 %copy-start.2 = (f32[16,1,128,128]{3,2,1,0:T(8,128)S(1)}, f32[16,1,128,128]{3,2,1,0:T(8,128)}, u32[]{:S(2)}) copy-start(f32[16,1,128,128]{3,2,1,0:T(8,128)} %param.15) | copy-start | bytes 3145732
  17.0 5.2 %copy-start.4 = (bf16[8,16,512]{2,1,0:T(8,128)(2,1)S(1)}, bf16[8,16,512]{2,1,0:T(8,128)(2,1)}, u32[]{:S(2)}) copy-start(bf16[8,16,512]{2,1,0:T(8,128)(2,1)} %param.8) | copy-start | bytes 393220
  17.0 5.2 %copy-start.5 = (bf16[2048,1]{0,1:T(2,128)(2,1)S(1)}, bf16[2048,1]{0,1:T(2,128)(2,1)}, u32[]{:S(2)}) copy-start(bf16[2048,1]{0,1:T(2,128)(2,1)} %param.10) | copy-start | bytes 12292
  17.0 5.2 %copy-start.6 = (f32[128]{0:T(128)S(1)}, f32[128]{0:T(128)}, u32[]{:S(2)}) copy-start(f32[128]{0:T(128)} %param.12) | copy-start | bytes 1540
  24.1 5.2 %collective-permute-start.3 = (f32[136,128]{1,0:T(8,128)S(1)}, f32[136,128]{1,0:T(8,128)S(1)}, u32[]{:S(2)}, u32[]{:S(2)}) collective-permute-start(f32[136,128]{1,0:T(8,128)S(1)} %shard_map.83.refs_0_), channel_id=1, source_target_pairs={{0,1},{1,0},{2,3},{3,2},{4,5},{5,4},{6,7},{7,6},{8,9},{9,8},{10,11... | collective-permute-start | bytes 208904 | tf_op jit(solution)/shard_map/ppermute | solution.py:43
  26.8 8.5 %collective-permute-start.4 = (f32[136,128]{1,0:T(8,128)S(1)}, f32[136,128]{1,0:T(8,128)S(1)}, u32[]{:S(2)}, u32[]{:S(2)}) collective-permute-start(f32[136,128]{1,0:T(8,128)S(1)} %shard_map.83.refs_0_), channel_id=1, source_target_pairs={{0,2},{1,3},{2,0},{3,1},{4,6},{5,7},{6,4},{7,5},{8,10},{9,11},{10,... | collective-permute-start | bytes 208904 | tf_op jit(solution)/shard_map/ppermute | solution.py:43
  28.0 7.4 %collective-permute-start.5 = (f32[136,128]{1,0:T(8,128)S(1)}, f32[136,128]{1,0:T(8,128)S(1)}, u32[]{:S(2)}, u32[]{:S(2)}) collective-permute-start(f32[136,128]{1,0:T(8,128)S(1)} %shard_map.83.refs_0_), channel_id=1, source_target_pairs={{0,3},{1,2},{2,1},{3,0},{4,7},{5,6},{6,5},{7,4},{8,11},{9,10},{10,... | collective-permute-start | bytes 208904 | tf_op jit(solution)/shard_map/ppermute | solution.py:43
where the time goes:
time: 36.6 us; the launch traced here: 36.4 us
  starting transfers between devices  15.4 us (42%)
  waiting for transfers between devices  13.3 us (36%)
  local copies, waits for them, and re-layouts  3.62 us (10%)
  Pallas kernels  3.38 us (9%)
  between operations  0.72 us (2%)
    ppermute x9, starting transfers between devices, exchange(): lax.ppermute(arrays[s], 'head', [(i, partner(i, s, size)) for i in range(...  15.3 us
    ppermute x9, waiting for transfers between devices, exchange(): lax.ppermute(arrays[s], 'head', [(i, partner(i, s, size)) for i in range(...  13.3 us
    unnamed x14, local copies, waits for them, and re-layouts  3.62 us
    pallas_call x1, Pallas kernels, local(): call(functools.partial(mesa_kernel, shards, steps), jax.ShapeDtypeStruct(...  1.96 us
    pallas_call x1, Pallas kernels, local(): call(functools.partial(output_kernel, shards), jax.ShapeDtypeStruct((rows...  1.05 us
  transfers between devices with their start and end apart: 10, of which 4 were waited for; matrix products, arithmetic and copies ran while one was open for 0% of the time, Pallas kernels for 6%

commit v1 on v0

--- a/solution.py
+++ b/solution.py
@@ -84,7 +84,7 @@
 
 def mesa_kernel(shards, steps, *refs):
     x_refs = refs[:shards]
-    w_ref, gate_ref, bias_ref, gain_ref, gram_ref, memory_ref, out_ref, kq, ab, xs, ys = refs[shards:]
+    w_ref, gate_ref, bias_ref, gain_ref, gram_ref, memory_ref, out_ref, wire_ref, kq, ab, xs, ys = refs[shards:]
     rows, features = x_refs[0].shape
     seqs = rows // steps
     size = out_ref.shape[1]
@@ -147,31 +147,35 @@
         y = ys[t * seqs : (t + 1) * seqs, :]
         for s in range(t + 1):
             y = y + scaled[s] * lane_sum(k[s] * b[t])
-        out_ref[t * seqs : (t + 1) * seqs, :] = y
-    out_ref[rows:, :] = jnp.broadcast_to(gain_ref[...], (out_ref.shape[0] - rows, size))
+        ys[t * seqs : (t + 1) * seqs, :] = y
+    readout = ys[...]
+    gained = gain_ref[...] * readout
+    out_ref[...] = gained
+    wire_ref[:rows] = gained.astype(jnp.bfloat16)
+    ones = jnp.ones((wire_ref.shape[0] - rows, size), jnp.bfloat16)
+    high, low = split(readout * readout)
+    high, low = split(dot(ones, high, ((1,), (1,))) + dot(ones, low, ((1,), (1,))))
+    row = lax.broadcasted_iota(jnp.int32, high.shape, 0)
+    terms = jnp.where(row == 0, high.astype(jnp.float32), jnp.where(row == 1, low.astype(jnp.float32), 0.0))
+    wire_ref[rows:] = terms.astype(jnp.bfloat16)
 
 
 def output_kernel(shards, *refs):
-    r_refs = refs[:shards]
-    own_ref = refs[shards]
-    mine_ref, other_ref, out_ref, w_scr = refs[shards + 1 :]
-    rows = out_ref.shape[0]
+    wire_refs = refs[:shards]
+    own_ref, w_own_ref, mine_ref, other_ref, out_ref, w_scr = refs[shards:]
+    rows, size = own_ref.shape
     half = mine_ref.shape[0] // (shards - 1)
-    width = own_ref.shape[0]
     mine = pl.multiple_of((lax.axis_index("batch") % 2) * half, half)
     other = pl.multiple_of(half - mine, half)
-    w_scr[:width] = own_ref[...]
     for s in range(1, shards):
-        w_scr[pl.ds(s * width + mine, half), :] = mine_ref[(s - 1) * half : s * half]
-        w_scr[pl.ds(s * width + other, half), :] = other_ref[(s - 1) * half : s * half]
-    size = r_refs[0].shape[1]
-    total = 0.0
-    for s in range(shards):
-        r = r_refs[s][:rows]
-        total = total + lane_sum(r * r)
+        w_scr[pl.ds((s - 1) * size + mine, half), :] = mine_ref[(s - 1) * half : s * half]
+        w_scr[pl.ds((s - 1) * size + other, half), :] = other_ref[(s - 1) * half : s * half]
+    terms = jnp.concatenate([ref[rows:] for ref in wire_refs], axis=0)
+    total = dot(terms, jnp.ones((terms.shape[0], size), jnp.bfloat16), ((0,), (0,)))
     scale = lax.rsqrt(total / (size * shards) + EPS)
-    hidden = [(r[rows : rows + 1] * r[:rows] * scale).astype(jnp.bfloat16) for r in r_refs]
-    out_ref[...] = dot(jnp.concatenate(hidden, axis=1), w_scr[...])
+    theirs = dot(jnp.concatenate([ref[:rows] for ref in wire_refs[1:]], axis=1), w_scr[...])
+    ours = dot((own_ref[...] * scale).astype(jnp.bfloat16), w_own_ref[...])
+    out_ref[...] = ours + theirs * jnp.concatenate([scale] * (out_ref.shape[1] // size), axis=1)
 
 
 def local(inputs, in_weight, gate_weight, gate_bias, norm_gain, out_weight, inv_gram, value_key):
@@ -197,19 +201,22 @@
     gram, memory = call(pack_kernel, (tiles, tiles))(
         inv_gram.reshape(seqs, size, size), value_key.reshape(seqs, size, size)
     )
-    readout = call(
+    readout, wire = call(
         functools.partial(mesa_kernel, shards, steps),
-        jax.ShapeDtypeStruct((rows + 8, size), jnp.float32),
+        (
+            jax.ShapeDtypeStruct((rows, size), jnp.float32),
+            jax.ShapeDtypeStruct((rows + 16, size), jnp.bfloat16),
+        ),
         [((2 * rows, size), jnp.float32)] * 2 + [((rows, size), jnp.float32)] * 2,
     )(*xs, weight, gate_weight.reshape(1, d_model), gate_bias.reshape(1, 1), norm_gain.reshape(1, size), gram, memory)
-    rs = [readout] + exchange([readout] * shards, shards)
+    rs = [wire] + exchange([wire] * shards, shards)
     w_mine = call(join_kernel, jax.ShapeDtypeStruct(((shards - 1) * half, out_cols), jnp.bfloat16))(*ws)
     w_other = lax.ppermute(w_mine, "batch", [(i, i ^ 1) for i in range(groups)])
     out = call(
         functools.partial(output_kernel, shards),
         jax.ShapeDtypeStruct((rows, out_cols), jnp.float32),
-        [((shards * size, out_cols), jnp.bfloat16)],
-    )(*rs, w_own, w_mine, w_other)
+        [(((shards - 1) * size, out_cols), jnp.bfloat16)],
+    )(*rs, readout, w_own, w_mine, w_other)
     return out.reshape(steps, seqs, out_cols)
 
 

time: 36.6 us -> 39.6 us (1.082)
  waiting for transfers between devices: 13.3 us -> 15.8 us
    ppermute x9, waiting for transfers between devices: 13.3 us -> 15.8 us  [exchange(): lax.ppermute(arrays[s], 'head', [(i, partner(i, s, size)) for i in range(...]
  transfers between devices with their start and end apart: 10 -> 10, of which waited for: 4 -> 6; matrix products, arithmetic and copies ran while one was open for 0% -> 0% of each run, Pallas kernels for 6% -> 6%
where the time goes in v1:
time: 39.6 us; the launch traced here: 39.4 us
  waiting for transfers between devices  15.8 us (40%)
  starting transfers between devices  15.7 us (40%)
  local copies, waits for them, and re-layouts  3.62 us (9%)
  Pallas kernels  3.52 us (9%)
  between operations  0.72 us (2%)
    ppermute x9, waiting for transfers between devices, exchange(): lax.ppermute(arrays[s], 'head', [(i, partner(i, s, size)) for i in range(...  15.8 us
    ppermute x9, starting transfers between devices, exchange(): lax.ppermute(arrays[s], 'head', [(i, partner(i, s, size)) for i in range(...  15.7 us
    unnamed x14, local copies, waits for them, and re-layouts  3.62 us
    pallas_call x1, Pallas kernels, local(): call(functools.partial(mesa_kernel, shards, steps), (jax.ShapeDtypeStruct...  2.1 us
    pallas_call x1, Pallas kernels, local(): call(functools.partial(output_kernel, shards), jax.ShapeDtypeStruct((rows...  1.05 us
  transfers between devices with their start and end apart: 10, of which 6 were waited for; matrix products, arithmetic and copies ran while one was open for 0% of the time, Pallas kernels for 6%

profile of v1, /device:TPU:0, one launch (start us, length us, event | category | flops | bytes accessed | tf_op | source)
XLA Modules:
  0.0 39.4 jit_solution(16963580218827861560)
XLA Ops:
  0.0 0.0 copy-start
  0.0 0.0 copy-start.3
  0.0 1.2 %copy-done.3 = bf16[128,2048]{1,0:T(8,128)(2,1)S(1)} copy-done((bf16[128,2048]{1,0:T(8,128)(2,1)S(1)}, bf16[128,2048]{1,0:T(8,128)(2,1)}, u32[]{:S(2)}) %copy-start.3) | copy-done | bytes 524312
  1.2 3.1 %collective-permute-start.6 = (bf16[64,512]{1,0:T(8,128)(2,1)S(1)}, bf16[64,512]{1,0:T(8,128)(2,1)S(1)}, u32[]{:S(2)}, u32[]{:S(2)}) collective-permute-start(bf16[64,512]{1,0:T(8,128)(2,1)S(1)} %get-tuple-element.18), channel_id=1, source_target_pairs={{0,1},{1,0},{2,3},{3,2},{4,5},{5,4},{6,7},{7,6},{8,9},{9,8},{10,11... | collective-permute-start | bytes 196616 | tf_op jit(solution)/shard_map/ppermute | solution.py:43
  4.3 2.6 %collective-permute-start.7 = (bf16[64,512]{1,0:T(8,128)(2,1)S(1)}, bf16[64,512]{1,0:T(8,128)(2,1)S(1)}, u32[]{:S(2)}, u32[]{:S(2)}) collective-permute-start(bf16[64,512]{1,0:T(8,128)(2,1)S(1)} %get-tuple-element.19), channel_id=1, source_target_pairs={{0,2},{1,3},{2,0},{3,1},{4,6},{5,7},{6,4},{7,5},{8,10},{9,11},{10,... | collective-permute-start | bytes 196616 | tf_op jit(solution)/shard_map/ppermute | solution.py:43
  6.9 0.0 collective-permute-start.8
  6.9 0.0 collective-permute-done.6.refs_0_
  6.9 4.7 %collective-permute-done.7.refs_1_ = bf16[64,512]{1,0:T(8,128)(2,1)S(1)} collective-permute-done((bf16[64,512]{1,0:T(8,128)(2,1)S(1)}, bf16[64,512]{1,0:T(8,128)(2,1)S(1)}, u32[]{:S(2)}, u32[]{:S(2)}) %collective-permute-start.7) | collective-permute-done | bytes 65568 | tf_op jit(solution)/shard_map/ppermute | solution.py:43
  11.6 1.4 %collective-permute-done.8.refs_2_ = bf16[64,512]{1,0:T(8,128)(2,1)S(1)} collective-permute-done((bf16[64,512]{1,0:T(8,128)(2,1)S(1)}, bf16[64,512]{1,0:T(8,128)(2,1)S(1)}, u32[]{:S(2)}, u32[]{:S(2)}) %collective-permute-start.8) | collective-permute-done | bytes 65568 | tf_op jit(solution)/shard_map/ppermute | solution.py:43
  13.0 0.1 collective-permute-start.9
  13.1 0.1 collective-permute-start
  13.2 2.3 %collective-permute-start.1 = (bf16[128,512]{1,0:T(8,128)(2,1)}, bf16[128,512]{1,0:T(8,128)(2,1)S(1)}, u32[]{:S(2)}, u32[]{:S(2)}) collective-permute-start(bf16[128,512]{1,0:T(8,128)(2,1)} %bitcast.13), channel_id=1, source_target_pairs={{0,2},{1,3},{2,0},{3,1},{4,6},{5,7},{6,4},{7,5},{8,10},{9,11},{10,... | collective-permute-start | bytes 393224 | tf_op jit(solution)/shard_map/ppermute | solution.py:43
  15.5 2.0 %collective-permute-start.2 = (bf16[128,512]{1,0:T(8,128)(2,1)}, bf16[128,512]{1,0:T(8,128)(2,1)S(1)}, u32[]{:S(2)}, u32[]{:S(2)}) collective-permute-start(bf16[128,512]{1,0:T(8,128)(2,1)} %bitcast.14), channel_id=1, source_target_pairs={{0,3},{1,2},{2,1},{3,0},{4,7},{5,6},{6,5},{7,4},{8,11},{9,10},{10,... | collective-permute-start | bytes 393224 | tf_op jit(solution)/shard_map/ppermute | solution.py:43
  18.2 0.0 copy-start.1
  18.2 1.2 %copy-done.1 = f32[16,1,128,128]{3,2,1,0:T(8,128)S(1)} copy-done((f32[16,1,128,128]{3,2,1,0:T(8,128)S(1)}, f32[16,1,128,128]{3,2,1,0:T(8,128)}, u32[]{:S(2)}) %copy-start.1) | copy-done | bytes 1048600
  19.4 0.0 copy-start.2
  19.4 1.2 %copy-done.2 = f32[16,1,128,128]{3,2,1,0:T(8,128)S(1)} copy-done((f32[16,1,128,128]{3,2,1,0:T(8,128)S(1)}, f32[16,1,128,128]{3,2,1,0:T(8,128)}, u32[]{:S(2)}) %copy-start.2) | copy-done | bytes 1048600
  20.6 0.0 copy-start.4
  20.6 0.0 copy-start.5
  20.6 0.0 copy-start.6
  20.6 0.3 shard_map.82
  21.0 0.8 %collective-permute-done.refs_1_ = bf16[128,512]{1,0:T(8,128)(2,1)S(1)} collective-permute-done((bf16[128,512]{1,0:T(8,128)(2,1)}, bf16[128,512]{1,0:T(8,128)(2,1)S(1)}, u32[]{:S(2)}, u32[]{:S(2)}) %collective-permute-start) | collective-permute-done | bytes 131104 | tf_op jit(solution)/shard_map/ppermute | solution.py:43
  21.8 4.6 %collective-permute-done.1.refs_2_ = bf16[128,512]{1,0:T(8,128)(2,1)S(1)} collective-permute-done((bf16[128,512]{1,0:T(8,128)(2,1)}, bf16[128,512]{1,0:T(8,128)(2,1)S(1)}, u32[]{:S(2)}, u32[]{:S(2)}) %collective-permute-start.1) | collective-permute-done | bytes 131104 | tf_op jit(solution)/shard_map/ppermute | solution.py:43
  26.4 0.0 collective-permute-done.2.refs_3_
  26.4 0.0 copy-done
  26.4 0.0 copy-done.4
  26.4 0.0 copy-done.5
  26.4 0.0 copy-done.6
  26.4 2.1 %shard_map.83 = (f32[128,128]{1,0:T(8,128)S(1)}, bf16[144,128]{1,0:T(8,128)(2,1)S(1)}) custom-call(bf16[128,512]{1,0:T(8,128)(2,1)S(1)} %bitcast.15, bf16[128,512]{1,0:T(8,128)(2,1)S(1)} %collective-permute-done.refs_1_, bf16[128,512]{1,0:T(8,128)(2,1)S(1)} %collective-permute-done.1.refs_2_, bf16[128,512]{1,0:T(8,128)(2,1)S(1)} %collective-permute-done.2.refs_3_, ...), custom_call_target="tpu_custom_call" | custom-call | tf_op jit(solution)/shard_map/pallas_call | solution.py:204
  28.5 2.8 %collective-permute-start.3 = (bf16[144,128]{1,0:T(8,128)(2,1)S(1)}, bf16[144,128]{1,0:T(8,128)(2,1)S(1)}, u32[]{:S(2)}, u32[]{:S(2)}) collective-permute-start(bf16[144,128]{1,0:T(8,128)(2,1)S(1)} %get-tuple-element.15.refs_0_), channel_id=1, source_target_pairs={{0,1},{1,0},{2,3},{3,2},{4,5},{5,4},{6,7},{7,6},{8,9},{9,8},{10,11... | collective-permute-start | bytes 110600 | tf_op jit(solution)/shard_map/ppermute | solution.py:43
  31.3 1.3 %collective-permute-start.4 = (bf16[144,128]{1,0:T(8,128)(2,1)S(1)}, bf16[144,128]{1,0:T(8,128)(2,1)S(1)}, u32[]{:S(2)}, u32[]{:S(2)}) collective-permute-start(bf16[144,128]{1,0:T(8,128)(2,1)S(1)} %get-tuple-element.15.refs_0_), channel_id=1, source_target_pairs={{0,2},{1,3},{2,0},{3,1},{4,6},{5,7},{6,4},{7,5},{8,10},{9,11},{10,... | collective-permute-start | bytes 110600 | tf_op jit(solution)/shard_map/ppermute | solution.py:43
  32.6 1.4 %collective-permute-start.5 = (bf16[144,128]{1,0:T(8,128)(2,1)S(1)}, bf16[144,128]{1,0:T(8,128)(2,1)S(1)}, u32[]{:S(2)}, u32[]{:S(2)}) collective-permute-start(bf16[144,128]{1,0:T(8,128)(2,1)S(1)} %get-tuple-element.15.refs_0_), channel_id=1, source_target_pairs={{0,3},{1,2},{2,1},{3,0},{4,7},{5,6},{6,5},{7,4},{8,11},{9,10},{10,... | collective-permute-start | bytes 110600 | tf_op jit(solution)/shard_map/ppermute | solution.py:43
  34.0 0.0 collective-permute-done.3.refs_1_
  34.0 2.9 %collective-permute-done.4.refs_2_ = bf16[144,128]{1,0:T(8,128)(2,1)S(1)} collective-permute-done((bf16[144,128]{1,0:T(8,128)(2,1)S(1)}, bf16[144,128]{1,0:T(8,128)(2,1)S(1)}, u32[]{:S(2)}, u32[]{:S(2)}) %collective-permute-start.4) | collective-permute-done | bytes 36896 | tf_op jit(solution)/shard_map/ppermute | solution.py:43
  36.9 1.4 %collective-permute-done.5.refs_3_ = bf16[144,128]{1,0:T(8,128)(2,1)S(1)} collective-permute-done((bf16[144,128]{1,0:T(8,128)(2,1)S(1)}, bf16[144,128]{1,0:T(8,128)(2,1)S(1)}, u32[]{:S(2)}, u32[]{:S(2)}) %collective-permute-start.5) | collective-permute-done | bytes 36896 | tf_op jit(solution)/shard_map/ppermute | solution.py:43
  38.4 0.0 collective-permute-done.9.refs_7_
  38.4 1.0 %shard_map.86 = f32[128,512]{1,0:T(8,128)} custom-call(bf16[144,128]{1,0:T(8,128)(2,1)S(1)} %get-tuple-element.15.refs_0_, bf16[144,128]{1,0:T(8,128)(2,1)S(1)} %collective-permute-done.3.refs_1_, bf16[144,128]{1,0:T(8,128)(2,1)S(1)} %collective-permute-done.4.refs_2_, bf16[144,128]{1,0:T(8,128)(2,1)S(1)} %collective-permute-done.5.refs_3_, ...), custom_call_target="tpu_custom_call" | custom-call | tf_op jit(solution)/shard_map/pallas_call | solution.py:215
  (2 shorter events, 0.0 us)
Async XLA Ops:
  0.0 26.4 %copy-start = (bf16[2048,1,384]{2,0,1:T(8,128)(2,1)S(1)}, bf16[2048,1,384]{2,0,1:T(8,128)(2,1)}, u32[]{:S(2)}) copy-start(bf16[2048,1,384]{2,0,1:T(8,128)(2,1)} %param.9) | copy-start | bytes 4718596
  0.0 1.2 %copy-start.3 = (bf16[128,2048]{1,0:T(8,128)(2,1)S(1)}, bf16[128,2048]{1,0:T(8,128)(2,1)}, u32[]{:S(2)}) copy-start(bf16[128,2048]{1,0:T(8,128)(2,1)} %weight_ref.1) | copy-start | bytes 1572868
  1.2 5.7 %collective-permute-start.6 = (bf16[64,512]{1,0:T(8,128)(2,1)S(1)}, bf16[64,512]{1,0:T(8,128)(2,1)S(1)}, u32[]{:S(2)}, u32[]{:S(2)}) collective-permute-start(bf16[64,512]{1,0:T(8,128)(2,1)S(1)} %get-tuple-element.18), channel_id=1, source_target_pairs={{0,1},{1,0},{2,3},{3,2},{4,5},{5,4},{6,7},{7,6},{8,9},{9,8},{10,11... | collective-permute-start | bytes 196616 | tf_op jit(solution)/shard_map/ppermute | solution.py:43
  4.3 7.3 %collective-permute-start.7 = (bf16[64,512]{1,0:T(8,128)(2,1)S(1)}, bf16[64,512]{1,0:T(8,128)(2,1)S(1)}, u32[]{:S(2)}, u32[]{:S(2)}) collective-permute-start(bf16[64,512]{1,0:T(8,128)(2,1)S(1)} %get-tuple-element.19), channel_id=1, source_target_pairs={{0,2},{1,3},{2,0},{3,1},{4,6},{5,7},{6,4},{7,5},{8,10},{9,11},{10,... | collective-permute-start | bytes 196616 | tf_op jit(solution)/shard_map/ppermute | solution.py:43
  6.9 6.1 %collective-permute-start.8 = (bf16[64,512]{1,0:T(8,128)(2,1)S(1)}, bf16[64,512]{1,0:T(8,128)(2,1)S(1)}, u32[]{:S(2)}, u32[]{:S(2)}) collective-permute-start(bf16[64,512]{1,0:T(8,128)(2,1)S(1)} %get-tuple-element.20), channel_id=1, source_target_pairs={{0,3},{1,2},{2,1},{3,0},{4,7},{5,6},{6,5},{7,4},{8,11},{9,10},{10,... | collective-permute-start | bytes 196616 | tf_op jit(solution)/shard_map/ppermute | solution.py:43
  13.0 25.4 %collective-permute-start.9 = (bf16[192,512]{1,0:T(8,128)(2,1)S(1)}, bf16[192,512]{1,0:T(8,128)(2,1)S(1)}, u32[]{:S(2)}, u32[]{:S(2)}) collective-permute-start(bf16[192,512]{1,0:T(8,128)(2,1)S(1)} %shard_map.85.refs_6_), channel_id=1, source_target_pairs={{0,4},{4,0},{8,12},{12,8},{16,20},{20,16},{24,28},{28,24},{1,5},{5... | collective-permute-start | bytes 589832 | tf_op jit(solution)/shard_map/ppermute | solution.py:214
  13.1 8.7 %collective-permute-start = (bf16[128,512]{1,0:T(8,128)(2,1)}, bf16[128,512]{1,0:T(8,128)(2,1)S(1)}, u32[]{:S(2)}, u32[]{:S(2)}) collective-permute-start(bf16[128,512]{1,0:T(8,128)(2,1)} %bitcast.12), channel_id=1, source_target_pairs={{0,1},{1,0},{2,3},{3,2},{4,5},{5,4},{6,7},{7,6},{8,9},{9,8},{10,11... | collective-permute-start | bytes 393224 | tf_op jit(solution)/shard_map/ppermute | solution.py:43
  13.2 13.2 %collective-permute-start.1 = (bf16[128,512]{1,0:T(8,128)(2,1)}, bf16[128,512]{1,0:T(8,128)(2,1)S(1)}, u32[]{:S(2)}, u32[]{:S(2)}) collective-permute-start(bf16[128,512]{1,0:T(8,128)(2,1)} %bitcast.13), channel_id=1, source_target_pairs={{0,2},{1,3},{2,0},{3,1},{4,6},{5,7},{6,4},{7,5},{8,10},{9,11},{10,... | collective-permute-start | bytes 393224 | tf_op jit(solution)/shard_map/ppermute | solution.py:43
  15.5 10.9 %collective-permute-start.2 = (bf16[128,512]{1,0:T(8,128)(2,1)}, bf16[128,512]{1,0:T(8,128)(2,1)S(1)}, u32[]{:S(2)}, u32[]{:S(2)}) collective-permute-start(bf16[128,512]{1,0:T(8,128)(2,1)} %bitcast.14), channel_id=1, source_target_pairs={{0,3},{1,2},{2,1},{3,0},{4,7},{5,6},{6,5},{7,4},{8,11},{9,10},{10,... | collective-permute-start | bytes 393224 | tf_op jit(solution)/shard_map/ppermute | solution.py:43
  18.2 1.2 %copy-start.1 = (f32[16,1,128,128]{3,2,1,0:T(8,128)S(1)}, f32[16,1,128,128]{3,2,1,0:T(8,128)}, u32[]{:S(2)}) copy-start(f32[16,1,128,128]{3,2,1,0:T(8,128)} %param.14) | copy-start | bytes 3145732
  19.4 1.2 %copy-start.2 = (f32[16,1,128,128]{3,2,1,0:T(8,128)S(1)}, f32[16,1,128,128]{3,2,1,0:T(8,128)}, u32[]{:S(2)}) copy-start(f32[16,1,128,128]{3,2,1,0:T(8,128)} %param.15) | copy-start | bytes 3145732
  20.6 5.7 %copy-start.4 = (bf16[8,16,512]{2,1,0:T(8,128)(2,1)S(1)}, bf16[8,16,512]{2,1,0:T(8,128)(2,1)}, u32[]{:S(2)}) copy-start(bf16[8,16,512]{2,1,0:T(8,128)(2,1)} %param.8) | copy-start | bytes 393220
  20.6 5.7 %copy-start.5 = (bf16[2048,1]{0,1:T(2,128)(2,1)S(1)}, bf16[2048,1]{0,1:T(2,128)(2,1)}, u32[]{:S(2)}) copy-start(bf16[2048,1]{0,1:T(2,128)(2,1)} %param.10) | copy-start | bytes 12292
  20.6 5.8 %copy-start.6 = (f32[128]{0:T(128)S(1)}, f32[128]{0:T(128)}, u32[]{:S(2)}) copy-start(f32[128]{0:T(128)} %param.12) | copy-start | bytes 1540
  28.5 5.5 %collective-permute-start.3 = (bf16[144,128]{1,0:T(8,128)(2,1)S(1)}, bf16[144,128]{1,0:T(8,128)(2,1)S(1)}, u32[]{:S(2)}, u32[]{:S(2)}) collective-permute-start(bf16[144,128]{1,0:T(8,128)(2,1)S(1)} %get-tuple-element.15.refs_0_), channel_id=1, source_target_pairs={{0,1},{1,0},{2,3},{3,2},{4,5},{5,4},{6,7},{7,6},{8,9},{9,8},{10,11... | collective-permute-start | bytes 110600 | tf_op jit(solution)/shard_map/ppermute | solution.py:43
  31.3 5.6 %collective-permute-start.4 = (bf16[144,128]{1,0:T(8,128)(2,1)S(1)}, bf16[144,128]{1,0:T(8,128)(2,1)S(1)}, u32[]{:S(2)}, u32[]{:S(2)}) collective-permute-start(bf16[144,128]{1,0:T(8,128)(2,1)S(1)} %get-tuple-element.15.refs_0_), channel_id=1, source_target_pairs={{0,2},{1,3},{2,0},{3,1},{4,6},{5,7},{6,4},{7,5},{8,10},{9,11},{10,... | collective-permute-start | bytes 110600 | tf_op jit(solution)/shard_map/ppermute | solution.py:43
  32.6 5.8 %collective-permute-start.5 = (bf16[144,128]{1,0:T(8,128)(2,1)S(1)}, bf16[144,128]{1,0:T(8,128)(2,1)S(1)}, u32[]{:S(2)}, u32[]{:S(2)}) collective-permute-start(bf16[144,128]{1,0:T(8,128)(2,1)S(1)} %get-tuple-element.15.refs_0_), channel_id=1, source_target_pairs={{0,3},{1,2},{2,1},{3,0},{4,7},{5,6},{6,5},{7,4},{8,11},{9,10},{10,... | collective-permute-start | bytes 110600 | tf_op jit(solution)/shard_map/ppermute | solution.py:43
